TPU v7x, 32 devices: a whole 2x2x4 slice. The times are simulated.
32 devices in a mesh: fit: 4 (over z), pair: 8 (over y, x, core).
Axes of the slice: x: 2, y: 2, z: 4, core: 2. Of those that a mesh axis runs over, the one named last changes fastest.
Arguments:
- metric_factor: bfloat16 [4096, 4096], P('fit'), as said below
- three_index: bfloat16 [4096, 16384], P('fit', 'pair'), may hold values from -6 to 6
- send_map: int32 [8, 8, 16], P('pair'), may hold values from 0 to 15
- pair_slots: int32 [8, 128], P('pair'), may hold values from 0 to 127, each once within a row
- pair_count: int32 [8], P('pair'), may hold values from 1 to 64, 256 in all
- orbital_energy: bfloat16 [128], P('pair'), may hold values from -2 to -0.19921875
- cabs_energy: float32 [1024], replicated, may hold values from 0.5 to 4
- coupling: bfloat16 [128, 1024], replicated, may hold values from -0.5 to 0.5
Outputs:
- projected: bfloat16 [8, 64, 128, 1024], P('pair', 'fit')
Inputs may be any that keep to these rules, and one draw needn't show every extreme that they name: `metric_factor`: diagonal entries lie between 0.6 and 1.4. `pair_slots`: each row holds every position 0 to 127 once; pair n of a row uses entries 2n and 2n + 1.
All inputs are finite; a program needn't handle non-finite values. No bound on the sum of `pair_count` on one device may be relied on, other than what follows from the above.
Results may differ from a plain program's by a relative error of at most 0.015.
Values may be sent and summed in bfloat16 or wider, within the bound.
No kernel may reach another device: no remote copies, remote signals or barrier semaphores. Data moves between devices by JAX's collectives and lax.ppermute only.
A program may use at most 256 MiB of HBM per device.

v0:
```python
import jax
import jax.numpy as jnp
from jax import lax
from jax.sharding import PartitionSpec as P

NAUX = 4096
PAIR_BLOCK = 8


def on_device(
    metric_factor,
    three_index,
    send_map,
    pair_slots,
    pair_count,
    orbital_energy,
    cabs_energy,
    coupling,
):
    domain = coupling.shape[0]
    orbitals = orbital_energy.shape[0]
    local_rows = metric_factor.shape[0]
    peers = send_map.shape[1]
    capacity = send_map.shape[2]
    slot_total = pair_slots.shape[1] // 2
    fitted = jnp.dot(
        metric_factor,
        lax.all_gather(three_index, "fit", axis=0, tiled=True),
        preferred_element_type=jnp.float32,
    )
    fitted = fitted.astype(jnp.bfloat16).reshape(local_rows, orbitals, domain)
    requests = send_map.reshape(peers, capacity)
    source, energy_src = (
        lax.all_gather(fitted, "pair", axis=1, tiled=True),
        lax.all_gather(orbital_energy, "pair", axis=0, tiled=True),
    )
    global_ids = (jnp.arange(peers, dtype=jnp.int32)[:, None] * orbitals + requests).reshape(-1)
    pair_index = jnp.take(global_ids, pair_slots[0])
    left_index = pair_index[0::2]
    right_index = pair_index[1::2]
    live_count = pair_count[0]
    norm_scale = NAUX ** (-0.5)
    block_count = (live_count + PAIR_BLOCK - 1) // PAIR_BLOCK

    def advance(block, partial_value):
        left_ids = lax.dynamic_slice_in_dim(left_index, block * PAIR_BLOCK, PAIR_BLOCK)
        right_ids = lax.dynamic_slice_in_dim(right_index, block * PAIR_BLOCK, PAIR_BLOCK)
        left_rows = jnp.take(source, left_ids, axis=1)
        right_rows = jnp.take(source, right_ids, axis=1)
        product = jnp.einsum(
            "qsa,qsb->sab", left_rows, right_rows, preferred_element_type=jnp.float32
        )
        return lax.dynamic_update_slice_in_dim(
            partial_value, product * norm_scale, block * PAIR_BLOCK, 0
        )

    partial_value = jnp.zeros((slot_total, domain, domain), jnp.float32)
    partial_value = lax.fori_loop(0, block_count, advance, partial_value)
    share = slot_total // lax.axis_size("fit")
    first_slot = lax.axis_index("fit") * share
    totals = lax.psum(partial_value.astype(jnp.bfloat16), "fit").astype(jnp.float32)
    exchange = lax.dynamic_slice_in_dim(totals, first_slot, share, 0)
    energy_sum = jnp.take(energy_src, left_index).astype(jnp.float32) + jnp.take(
        energy_src, right_index
    ).astype(jnp.float32)
    energy_sum = lax.dynamic_slice_in_dim(energy_sum, first_slot, share, 0)
    weighted = jnp.einsum(
        "sab,bc->sac", exchange.astype(jnp.bfloat16), coupling, preferred_element_type=jnp.float32
    )
    denom = cabs_energy[None, None, :] - energy_sum[:, None, None]
    live_mask = first_slot + jnp.arange(share, dtype=jnp.int32) < live_count
    projected = jnp.where(live_mask[:, None, None], weighted / denom, 0.0).astype(jnp.bfloat16)
    return projected.reshape(1, share, domain, weighted.shape[2])


def solution(mesh):
    in_specs = (
        P("fit", None),
        P("fit", "pair"),
        P("pair", None, None),
        P("pair", None),
        P("pair"),
        P("pair"),
        P(),
        P(),
    )
    out_specs = P("pair", "fit", None, None)
    return jax.shard_map(
        on_device, mesh=mesh, in_specs=in_specs, out_specs=out_specs, check_vma=False
    )
```

profile of v0, /device:TPU:0, one launch (start us, length us, event | category | flops | bytes accessed | tf_op | source)
XLA Modules:
  0.0 655.6 jit_solution(15301180865822851365)
XLA Ops:
  6.5 0.0 copy-start
  6.5 0.0 all-gather.3.cloned.1.call-start
  6.5 0.7 all-gather.3.cloned.1.call-update
  7.3 0.0 all-gather.5.cloned.1.call-start
  7.3 291.1 %all-gather.3.cloned.1.call-done = bf16[4096,2048]{1,0:T(8,128)(2,1)} async-done(((bf16[1024,2048]{1,0:T(8,128)(2,1)}), bf16[4096,2048]{1,0:T(8,128)(2,1)}) %all-gather.3.cloned.1.call-update) | async-done | bytes 16777232 | tf_op jit(solution)/shard_map/all_gather | solution.py:28
  298.4 22.7 %convert_bitcast_fusion = bf16[128,16,8,128]{3,2,1,0:T(8,128)(2,1)S(1)} fusion(bf16[1024,4096]{1,0:T(8,128)(2,1)} %param.14, bf16[4096,2048]{1,0:T(8,128)(2,1)} %all-gather.3.cloned.1.call-done), kind=kOutput, calls=%fused_computation.24 | convolution fusion | flops 17181966336 | bytes 29360128 | tf_op jit(solution)/shard_map/dot_general | solution.py:26
  321.1 3.1 copy.18
  324.2 0.0 copy-start.2
  324.2 0.0 copy-start.3
  324.2 0.0 all-gather.5.cloned.1.call-update
  324.2 0.0 all-reduce.3.cloned.1.call-start
  325.0 0.1 add.77
  325.0 0.1 add.78
  325.1 0.0 copy-done.2
  325.1 0.1 reshape.94
  325.2 0.0 copy-done.3
  325.2 1.2 gather_fusion.2
  326.5 0.2 slice.6
  326.6 0.2 slice.7
  326.8 156.4 %all-gather.5.cloned.1.call-done = bf16[1024,128,128]{2,0,1:T(8,128)(2,1)} async-done(((bf16[1024,16,128]{2,0,1:T(8,128)(2,1)}), bf16[1024,128,128]{2,0,1:T(8,128)(2,1)}) %all-gather.5.cloned.1.call-update) | async-done | bytes 33554448 | tf_op jit(solution)/shard_map/all_gather | solution.py:34
  483.2 1.8 broadcast_in_dim.41
  485.1 9.2 %while.10 = (s32[]{:T(128)}, bf16[64,128,128]{2,1,0:T(8,128)(2,1)}, s32[]{:T(128)}, s32[64]{0:T(128)S(1)}, bf16[1024,128,128]{2,0,1:T(8,128)(2,1)}, /*index=5*/s...) while((s32[]{:T(128)}, bf16[64,128,128]{2,1,0:T(8,128)(2,1)}, s32[]{:T(128)}, s32[64]{0:T(128)S(1)}, ...), condition=%wide.region_1.3_spmd, body=%wide.region_0.0_spmd.sunk | while | flops 270665824 | bytes 13115835 | solution.py:58
  485.1 0.1 compare_and_fusion.3
  485.2 2.4 gather_fusion
  487.5 3.5 gather_fusion.1
  491.1 3.2 fusion.31
  494.3 0.0 copy-start.5
  494.3 0.0 copy-start.4
  494.3 0.0 copy-start.1
  494.3 0.0 all-reduce.3.cloned.1.call-update
  494.3 0.6 copy-done.5
  495.0 0.6 dynamic-slice
  496.3 0.0 copy-done.4
  496.3 0.2 dynamic-update-slice
  496.6 77.8 %all-reduce = bf16[128]{0:T(256)(128)(2,1)S(1)} all-reduce(bf16[128]{0:T(256)(128)(2,1)S(1)} %dynamic-update-slice), channel_id=1, replica_groups=mesh['fit'=4,'pair'=8] {'pair'}, use_global_device_ids=true, to_apply=%add | all-reduce | flops 128 | bytes 512
  574.3 0.8 gather_fusion.3
  575.1 0.8 gather_fusion.4
  575.9 0.1 dynamic_slice.13
  576.0 0.0 copy-done.1
  576.0 0.1 broadcast_subtract_fusion
  576.1 68.7 %all-reduce.3.cloned.1.call-done = bf16[64,128,128]{2,1,0:T(8,128)(2,1)} async-done(((bf16[64,128,128]{2,1,0:T(8,128)(2,1)}), bf16[64,128,128]{2,1,0:T(8,128)(2,1)}) %all-reduce.3.cloned.1.call-update) | async-done | bytes 2097168 | tf_op jit(solution)/shard_map/psum | solution.py:61
  644.8 0.0 copy-done
  644.8 4.3 fusion.19
  (14 shorter events, 0.1 us)
Async XLA Ops:
  6.5 638.2 %copy-start = (bf16[128,1024]{1,0:T(8,128)(2,1)S(1)}, bf16[128,1024]{1,0:T(8,128)(2,1)}, u32[]{:S(2)}) copy-start(bf16[128,1024]{1,0:T(8,128)(2,1)} %param.21) | copy-start | bytes 786436
  6.5 291.9 %all-gather.3.cloned.1.call-start = ((), (), s32[]{:S(2)}) async-start(), calls=%async_computation | async-start | bytes 20971520 | tf_op jit(solution)/shard_map/all_gather | solution.py:28
  7.3 476.0 %all-gather.5.cloned.1.call-start = ((), (), s32[]{:S(2)}) async-start(), calls=%async_computation.1 | async-start | bytes 37748736 | tf_op jit(solution)/shard_map/all_gather | solution.py:34
  324.2 0.9 copy-start.2
  324.2 1.0 copy-start.3
  324.2 320.5 %all-reduce.3.cloned.1.call-start = ((), (), s32[]{:S(2)}) async-start(), calls=%async_computation.2 | async-start | bytes 4194304 | tf_op jit(solution)/shard_map/psum | solution.py:61
  494.3 0.7 copy-start.5
  494.3 2.0 copy-start.4
  494.3 81.7 %copy-start.1 = (f32[1024]{0:T(1024)S(1)}, f32[1024]{0:T(1024)}, u32[]{:S(2)}) copy-start(f32[1024]{0:T(1024)} %param.20) | copy-start | bytes 12292
Sparse Core Ops, SparseCore 0:
  8.9 289.4 all-gather.2
  324.4 158.8 all-gather.4
  494.5 150.2 all-reduce.2
where the time goes:
time: 657 us; the launch traced here: 656 us
  waiting for transfers between devices  517 us (79%)
  blocking collectives  77.8 us (12%)
  matrix products  30.2 us (5%)
  local copies, waits for them, and re-layouts  15.8 us (2%)
  between operations  14.6 us (2%)
    all_gather x1, waiting for transfers between devices, on_device(): lax.all_gather(three_index, 'fit', axis=0, tiled=True)  291 us
    all_gather x1, waiting for transfers between devices, on_device(): lax.all_gather(fitted, 'pair', axis=1, tiled=True)  156 us
    unnamed x1, blocking collectives  77.8 us
    psum x1, waiting for transfers between devices, on_device(): lax.psum(partial_value.astype(jnp.bfloat16), 'fit').astype(jnp.float32)  68.7 us
    dot_general x1, matrix products, on_device(): jnp.dot(metric_factor, lax.all_gather(three_index, 'fit', axis=0, tiled=T...  22.7 us
  transfers between devices with their start and end apart: 3, of which 3 were waited for; matrix products, arithmetic and copies ran while one was open for 1% of the time, Pallas kernels for 0%

commit v1 on v0

--- a/solution.py
+++ b/solution.py
@@ -5,6 +5,12 @@
 
 NAUX = 4096
 PAIR_BLOCK = 8
+
+
+def summed_here(array, axis):
+    parts = lax.all_gather(array, axis, axis=0, tiled=False)
+    acc = parts.sum(axis=0)
+    return acc
 
 
 def on_device(
@@ -58,7 +64,7 @@
     partial_value = lax.fori_loop(0, block_count, advance, partial_value)
     share = slot_total // lax.axis_size("fit")
     first_slot = lax.axis_index("fit") * share
-    totals = lax.psum(partial_value.astype(jnp.bfloat16), "fit").astype(jnp.float32)
+    totals = summed_here(partial_value.astype(jnp.bfloat16), "fit").astype(jnp.float32)
     exchange = lax.dynamic_slice_in_dim(totals, first_slot, share, 0)
     energy_sum = jnp.take(energy_src, left_index).astype(jnp.float32) + jnp.take(
         energy_src, right_index

time: 657 us -> 725 us (1.10)
  waiting for transfers between devices: 517 us -> 581 us
    all_gather x0 -> x1, waiting for transfers between devices: none -> 133 us  [summed_here(): parts = lax.all_gather(array, axis, axis=0, tiled=False)]
    psum x1 -> x0, waiting for transfers between devices: 68.7 us -> none  [on_device(): lax.psum(partial_value.astype(jnp.bfloat16), 'fit').astype(jnp.float32)]
where the time goes in v1:
time: 725 us; the launch traced here: 724 us
  waiting for transfers between devices  581 us (80%)
  blocking collectives  77.4 us (11%)
  matrix products  29.2 us (4%)
  local copies, waits for them, and re-layouts  15.7 us (2%)
  between operations  14.5 us (2%)
    all_gather x1, waiting for transfers between devices, on_device(): lax.all_gather(three_index, 'fit', axis=0, tiled=True)  291 us
    all_gather x1, waiting for transfers between devices, on_device(): lax.all_gather(fitted, 'pair', axis=1, tiled=True)  156 us
    all_gather x1, waiting for transfers between devices, summed_here(): parts = lax.all_gather(array, axis, axis=0, tiled=False)  133 us
    unnamed x1, blocking collectives  77.4 us
    dot_general x1, matrix products, on_device(): jnp.dot(metric_factor, lax.all_gather(three_index, 'fit', axis=0, tiled=T...  22.7 us
  transfers between devices with their start and end apart: 3, of which 3 were waited for; matrix products, arithmetic and copies ran while one was open for 1% of the time, Pallas kernels for 0%

profile of v1, /device:TPU:0, one launch (start us, length us, event | category | flops | bytes accessed | tf_op | source)
XLA Modules:
  0.0 723.7 jit_solution(7343074045544064265)
XLA Ops:
  6.5 0.0 copy-start
  6.5 0.0 all-gather.5.cloned.1.call-start
  6.5 0.7 all-gather.5.cloned.1.call-update
  7.3 0.0 all-gather.7.cloned.1.call-start
  7.3 291.1 %all-gather.5.cloned.1.call-done = bf16[4096,2048]{1,0:T(8,128)(2,1)} async-done(((bf16[1024,2048]{1,0:T(8,128)(2,1)}), bf16[4096,2048]{1,0:T(8,128)(2,1)}) %all-gather.5.cloned.1.call-update) | async-done | bytes 16777232 | tf_op jit(solution)/shard_map/all_gather | solution.py:34
  298.4 22.7 %convert_bitcast_fusion = bf16[128,16,8,128]{3,2,1,0:T(8,128)(2,1)S(1)} fusion(bf16[1024,4096]{1,0:T(8,128)(2,1)} %param.14, bf16[4096,2048]{1,0:T(8,128)(2,1)} %all-gather.5.cloned.1.call-done), kind=kOutput, calls=%fused_computation.24 | convolution fusion | flops 17181966336 | bytes 29360128 | tf_op jit(solution)/shard_map/dot_general | solution.py:32
  321.1 3.1 copy.18
  324.2 0.0 copy-start.2
  324.2 0.0 copy-start.3
  324.2 0.0 all-gather.7.cloned.1.call-update
  324.2 0.0 all-gather.9.cloned.1.call-start
  324.9 0.1 add.75
  325.0 0.1 add.76
  325.1 0.0 copy-done.2
  325.1 0.1 reshape.94
  325.2 0.0 copy-done.3
  325.2 1.2 gather_fusion.2
  326.5 0.2 slice.6
  326.6 0.2 slice.7
  326.8 156.4 %all-gather.7.cloned.1.call-done = bf16[1024,128,128]{2,0,1:T(8,128)(2,1)} async-done(((bf16[1024,16,128]{2,0,1:T(8,128)(2,1)}), bf16[1024,128,128]{2,0,1:T(8,128)(2,1)}) %all-gather.7.cloned.1.call-update) | async-done | bytes 33554448 | tf_op jit(solution)/shard_map/all_gather | solution.py:40
  483.2 1.8 broadcast_in_dim.41
  485.1 9.2 %while.10 = (s32[]{:T(128)}, bf16[64,128,128]{2,1,0:T(8,128)(2,1)}, s32[]{:T(128)}, s32[64]{0:T(128)S(1)}, bf16[1024,128,128]{2,0,1:T(8,128)(2,1)}, /*index=5*/s...) while((s32[]{:T(128)}, bf16[64,128,128]{2,1,0:T(8,128)(2,1)}, s32[]{:T(128)}, s32[64]{0:T(128)S(1)}, ...), condition=%wide.region_1.3_spmd, body=%wide.region_0.0_spmd.sunk | while | flops 270665824 | bytes 13115835 | solution.py:64
  485.1 0.1 compare_and_fusion.3
  485.2 2.4 gather_fusion
  487.5 3.5 gather_fusion.1
  491.1 3.2 fusion.31
  494.3 0.0 copy-start.5
  494.3 0.0 copy-start.4
  494.3 0.0 copy-start.1
  494.3 0.0 all-gather.9.cloned.1.call-update
  494.3 0.6 copy-done.5
  495.0 0.6 dynamic-slice
  496.1 0.0 copy-done.4
  496.1 0.2 dynamic-update-slice
  496.4 77.4 %all-reduce = bf16[128]{0:T(256)(128)(2,1)S(1)} all-reduce(bf16[128]{0:T(256)(128)(2,1)S(1)} %dynamic-update-slice), channel_id=1, replica_groups=mesh['fit'=4,'pair'=8] {'pair'}, use_global_device_ids=true, to_apply=%add | all-reduce | flops 128 | bytes 512
  573.8 0.8 gather_fusion.3
  574.5 0.8 gather_fusion.4
  575.3 0.1 dynamic_slice.13
  575.4 0.0 copy-done.1
  575.4 0.1 broadcast_subtract_fusion
  575.5 132.7 %all-gather.9.cloned.1.call-done = bf16[256,128,128]{2,1,0:T(8,128)(2,1)} async-done(((bf16[64,128,128]{2,1,0:T(8,128)(2,1)}), bf16[256,128,128]{2,1,0:T(8,128)(2,1)}) %all-gather.9.cloned.1.call-update) | async-done | bytes 8388624 | tf_op jit(solution)/shard_map/all_gather | solution.py:11
  708.2 5.7 reduce_sum.12
  713.9 0.0 copy-done
  713.9 3.3 fusion.19
  (14 shorter events, 0.1 us)
Async XLA Ops:
  6.5 707.4 %copy-start = (bf16[128,1024]{1,0:T(8,128)(2,1)S(1)}, bf16[128,1024]{1,0:T(8,128)(2,1)}, u32[]{:S(2)}) copy-start(bf16[128,1024]{1,0:T(8,128)(2,1)} %param.21) | copy-start | bytes 786436
  6.5 291.9 %all-gather.5.cloned.1.call-start = ((), (), s32[]{:S(2)}) async-start(), calls=%async_computation | async-start | bytes 20971520 | tf_op jit(solution)/shard_map/all_gather | solution.py:34
  7.3 476.0 %all-gather.7.cloned.1.call-start = ((), (), s32[]{:S(2)}) async-start(), calls=%async_computation.1 | async-start | bytes 37748736 | tf_op jit(solution)/shard_map/all_gather | solution.py:40
  324.2 0.9 copy-start.2
  324.2 1.0 copy-start.3
  324.2 384.0 %all-gather.9.cloned.1.call-start = ((), (), s32[]{:S(2)}) async-start(), calls=%async_computation.2 | async-start | bytes 10485760 | tf_op jit(solution)/shard_map/all_gather | solution.py:11
  494.3 0.7 copy-start.5
  494.3 1.8 copy-start.4
  494.3 81.1 %copy-start.1 = (f32[1024]{0:T(1024)S(1)}, f32[1024]{0:T(1024)}, u32[]{:S(2)}) copy-start(f32[1024]{0:T(1024)} %param.20) | copy-start | bytes 12292
Sparse Core Ops, SparseCore 0:
  8.9 289.4 all-gather.4
  324.4 158.8 all-gather.6
  494.5 213.7 all-gather.8
